TPU v7x, 32 devices: a whole 2x2x4 slice. The times are simulated.
32 devices in a mesh: node: 16 (over z, y, core), blk: 2 (over x).
Axes of the slice: x: 2, y: 2, z: 4, core: 2. Of those that a mesh axis runs over, the one named last changes fastest.
Arguments:
- params: bfloat16 [16, 128, 14336], P('node', 'blk'), may hold values from -40 to 40
- weights: int32 [16], P('node'), may hold values from 1 to 8
Outputs:
- debiased: float32 [16, 128, 14336], P('node', 'blk')
- average: float32 [128, 14336], P('blk', 'node')
- spread: float32 [16], P('node')
All inputs are finite; a program needn't handle non-finite values.
Results may differ from a plain program's by a relative error of at most 0.0003.
Values may be sent and summed in bfloat16 or wider, within the bound.
A program may use at most 64 MiB of HBM per device.

v0:
```python
import functools

import jax
import jax.numpy as jnp
from jax import lax
from jax.experimental import pallas as pl
from jax.experimental.pallas import tpu as pltpu
from jax.sharding import PartitionSpec as P

ROUNDS = 3
GROUP = 4
LEVELS = 4
SPLIT = 4
LANES = 128
NEIGHBOUR = (1, 0, 3, 2)


def kernel(p_ref, w_ref, out_ref, avg_ref, spread_ref,
           raw_own, raw_a, raw_b, raw_c, q_a, q_b, q_send, dbuf, avgbuf,
           wts, acc, spread_in, spread_part, spread_x,
           near_send, near_recv, own_sem, far_send, far_recv, back_send, back_recv,
           back_own, w_send, w_recv, s_send, s_recv, avg_sem, fore_in, f_send, f_recv):
    node = lax.axis_index("node")
    side = lax.axis_index("blk")
    z = node // GROUP
    r = node % GROUP
    half, core = r // 2, r % 2
    rows, width = raw_own.shape[2], raw_own.shape[3]
    chunks = raw_own.shape[0]
    hidden = p_ref.shape[2]
    row_total = p_ref.shape[1] * lax.axis_size("blk")

    def peer(o):
        y = 1 - half if o & 2 else half
        c = 1 - core if o & 1 else core
        return y * 2 + c

    def dev(zz, rr):
        return {"node": zz * GROUP + rr}

    inner = jnp.logical_and(z >= 1, z <= 2)
    order = [k + half_of for k in range(chunks // 2) for half_of in (0, chunks // 2)]
    mate = 3 - z
    nb = (z // 2) * 2 + 1 - z % 2
    inner_count = (1 - z // 3) * ((z + 2) // 3)

    def remote(src, dst, ssem, rsem, device):
        return pltpu.make_async_remote_copy(
            src_ref=src, dst_ref=dst, send_sem=ssem, recv_sem=rsem,
            device_id=device, device_id_type=pl.DeviceIdType.MESH)

    wts[z, r] = jnp.full((8, LANES), w_ref[0].astype(jnp.float32))
    acc[...] = jnp.zeros_like(acc)

    def own_slice(k):
        return pl.ds((k % SPLIT) * rows, rows)

    def block(k, rr):
        return pl.ds(pl.multiple_of(((k // SPLIT) * GROUP + rr) * width, LANES), width)

    locals_in = []
    for k in range(chunks):
        locals_in.append(pltpu.make_async_copy(
            p_ref.at[0, own_slice(k), block(k, r)], raw_own.at[k, r], own_sem.at[k]))
        locals_in[-1].start()

    barrier = pltpu.get_barrier_semaphore()

    def greet(device):
        pl.semaphore_signal(barrier, inc=1, device_id=device,
                            device_id_type=pl.DeviceIdType.MESH)

    for o in (1, 2, 3):
        greet(dev(z, peer(o)))
    greet({"blk": 1 - side})
    greet(dev(nb, r))

    @pl.when(inner)
    def _():
        greet(dev(mate, r))

    pl.semaphore_wait(barrier, 5 + inner_count)

    def w_near(o):
        return remote(wts.at[z, r], wts.at[z, r], w_send.at[o - 1], w_recv.at[o - 1],
                      dev(z, peer(o)))

    def near(k, o):
        return remote(p_ref.at[0, own_slice(k), block(k, peer(o))], raw_own.at[k, r],
                      near_send.at[k, o - 1], near_recv.at[k, o - 1], dev(z, peer(o)))

    for o in (1, 2, 3):
        w_near(o).start()
    for k in order:
        for o in (2, 3, 1):
            near(k, o).start()

    arrived = set()

    def wait_own(k):
        if k in arrived:
            return
        arrived.add(k)
        locals_in[k].wait()
        for o in (1, 2, 3):
            near(k, o).wait_recv()

    def row(zz, i):
        return wts[zz, i, 0:1, :]

    def f32(ref, k, i, cols):
        return ref[k, i, :, cols].astype(jnp.float32)

    def group_sum(ref, k, zz, cols):
        total = f32(ref, k, 0, cols) * row(zz, 0)
        for i in range(1, GROUP):
            total = total + f32(ref, k, i, cols) * row(zz, i)
        return total

    def columns(j):
        return pl.ds(pl.multiple_of(j * LANES, LANES), LANES)

    def back(k, o):
        return remote(dbuf.at[k, peer(o)], out_ref.at[0, own_slice(k), block(k, r)],
                      back_send.at[k, o - 1], back_recv.at[k, o - 1], dev(z, peer(o)))

    def back_local(k):
        return pltpu.make_async_copy(
            dbuf.at[k, r], out_ref.at[0, own_slice(k), block(k, r)], back_own.at[k])

    def group_weight(zz):
        return row(zz, 0) + row(zz, 1) + row(zz, 2) + row(zz, 3)

    def scales_of(level):
        opp = (level + 2) % LEVELS
        sums = [group_weight((level + 3) % LEVELS)] * GROUP
        for i in range(GROUP):
            for e in range(GROUP):
                if e <= i:
                    sums[i] = sums[i] + row(level, e)
                else:
                    sums[i] = sums[i] + row(opp, e)
        return [1.0 / value for value in sums]

    def is_low(k):
        return k < chunks // 2

    def finish(k, level):
        is_inner = level in (1, 2)
        has_mean = is_low(k) == (level < 2)
        opp, beside, across_level = (level + 2) % 4, NEIGHBOUR[level], 3 - level
        if is_inner:
            raws = {level: raw_own, beside: raw_a, across_level: raw_b, opp: raw_c}
            group_refs = {}
        else:
            raws = {level: raw_own, opp: raw_a}
            group_refs = {beside: q_a, across_level: q_b}
        targets = [level]
        if is_inner and has_mean:
            targets += [across_level, opp]
        scales = {y: scales_of(y) for y in targets}
        whole = 1.0 / (group_weight(0) + group_weight(1) + group_weight(2) + group_weight(3))

        def step(j, sums):
            cols = columns(j)
            seen = {}

            def value(y, i):
                if (y, i) not in seen:
                    seen[y, i] = f32(raws[y], k, i, cols) * row(y, i)
                return seen[y, i]

            def group_of(y):
                if y not in seen:
                    if y in group_refs:
                        seen[y] = group_refs[y][k, :, cols]
                    else:
                        seen[y] = (value(y, 0) + value(y, 1)) + (value(y, 2) + value(y, 3))
                return seen[y]

            if is_inner and sends_opposite(level, k):
                q_send[k, 1, :, cols] = group_of(opp)
            if has_mean:
                mean = (group_of(0) + group_of(1) + group_of(2) + group_of(3)) * whole
                avgbuf[k // SPLIT, own_slice(k), cols] = mean
            fresh = []
            for n, y in enumerate(targets):
                far = (y + 2) % LEVELS
                prior = group_of((y + 3) % LEVELS)
                heads = [value(y, 0)]
                for i in range(1, GROUP):
                    heads.append(heads[-1] + value(y, i))
                tails = [None, None, None, value(far, 3)]
                for i in (2, 1):
                    tails[i] = tails[i + 1] + value(far, i)
                for i in range(GROUP):
                    d = heads[i] + prior
                    if i + 1 < GROUP:
                        d = d + tails[i + 1]
                    d = d * scales[y][i]
                    if n == 0:
                        dbuf[k, i, :, cols] = d
                    if has_mean:
                        gap = d - mean
                        gap = gap * gap
                        part = gap[0:8]
                        for e in range(8, rows, 8):
                            part = part + gap[e:e + 8]
                        fresh.append(sums[len(fresh)] + part)
            return tuple(fresh)

        zero = jnp.zeros((8, LANES), jnp.float32)
        count = GROUP * len(targets) if has_mean else 0
        sums = lax.fori_loop(0, width // LANES, step, (zero,) * count)
        for i in range(count):
            acc[i // GROUP, i % GROUP] += sums[i]

    def share(o):
        return remote(acc.at[0, peer(o)], spread_in.at[o - 1], s_send.at[o - 1],
                      s_recv.at[o - 1], dev(z, peer(o)))

    def send_back(k):
        for o in (2, 3, 1):
            back(k, o).start()
        back_local(k).start()

    def nodes(full):
        return pl.ds(0, GROUP) if full else pl.ds(1, GROUP - 1)

    def sends_opposite(level, k):
        return level == 1 or not is_low(k)

    def sends_own(level, k):
        return level == 2 or is_low(k)

    def to_inner(k, beside):
        return remote(raw_own.at[k], raw_a.at[k], far_send.at[k, 0], far_recv.at[k, 0],
                      dev(beside, r))

    def across(k, source):
        part = nodes(source == 1 or is_low(k))
        return remote(raw_own.at[k, part], raw_b.at[k, part], far_send.at[k, 0],
                      far_recv.at[k, 1], dev(3 - source, r))

    def across_relay(k, source):
        part = nodes(source == 2 or not is_low(k))
        return remote(raw_a.at[k, part], raw_c.at[k, part], far_send.at[k, 1],
                      far_recv.at[k, 2], dev(3 - source, r))

    def outward_relay(k, source):
        part = nodes(is_low(k) == (source == 1))
        return remote(raw_b.at[k, part], raw_a.at[k, part], far_send.at[k, 2],
                      far_recv.at[k, 0], dev(NEIGHBOUR[source], r))

    def outward_q(k, which, source):
        dst = q_b if which else q_a
        return remote(q_send.at[k, which], dst.at[k], far_send.at[k, 3 + which],
                      far_recv.at[k, 3 + which], dev(NEIGHBOUR[source], r))

    def w_copy(level, slot, target):
        return remote(wts.at[level], wts.at[level], w_send.at[slot], w_recv.at[slot],
                      dev(target, r))

    def wait_weights():
        for o in (1, 2, 3):
            w_near(o).wait_recv()

    def foreign(target):
        return remote(acc.at[pl.ds(1, 2)], fore_in, f_send.at[0], f_recv.at[0],
                      dev(target, r))

    def foreign_relay(target):
        return remote(fore_in.at[1], fore_in.at[0], f_send.at[1], f_recv.at[1],
                      dev(target, r))

    def inner_role(level):
        beside, other, opp = NEIGHBOUR[level], 3 - level, (level + 2) % LEVELS
        arrived.clear()

        def group_out(k):
            wait_own(k)
            if not sends_own(level, k):
                return

            def step(j, carry):
                cols = columns(j)
                q_send[k, 0, :, cols] = group_sum(raw_own, k, level, cols)
                return carry

            lax.fori_loop(0, width // LANES, step, 0)
            outward_q(k, 0, level).start()

        wait_weights()
        w_copy(level, 3, beside).start()
        w_copy(level, 4, other).start()
        for t in range(chunks + 2):
            if t < chunks:
                wait_own(order[t])
                across(order[t], level).start()
            for e in ((0,) if t == 0 else (2 * t - 1, 2 * t)):
                if e < chunks:
                    group_out(order[e])
            if t == 1:
                w_copy(beside, 3, beside).wait_recv()
                w_copy(beside, 5, other).start()
                w_copy(level, 4, other).wait_recv()
                w_copy(other, 6, beside).start()
            if 0 <= t - 1 < chunks:
                k = order[t - 1]
                to_inner(k, beside).wait_recv()
                across_relay(k, level).start()
                across(k, other).wait_recv()
                outward_relay(k, level).start()
            if t == 2:
                w_copy(opp, 5, other).wait_recv()
                w_copy(opp, 7, beside).start()
            if 0 <= t - 2 < chunks:
                k = order[t - 2]
                across_relay(k, other).wait_recv()
                finish(k, level)
                if sends_opposite(level, k):
                    outward_q(k, 1, level).start()
                if t == chunks + 1:
                    foreign(other).start()
                send_back(k)
        foreign(other).wait_recv()
        foreign_relay(beside).start()
        acc[0] += fore_in[0]
        for o in (1, 2, 3):
            share(o).start()
        for k in order:
            across(k, level).wait_send()
            across_relay(k, level).wait_send()
            outward_relay(k, level).wait_send()
            if sends_own(level, k):
                outward_q(k, 0, level).wait_send()
            if sends_opposite(level, k):
                outward_q(k, 1, level).wait_send()
        w_copy(level, 3, beside).wait_send()
        w_copy(level, 4, other).wait_send()
        w_copy(beside, 5, other).wait_send()
        w_copy(other, 6, beside).wait_send()
        w_copy(opp, 7, beside).wait_send()
        foreign(other).wait_send()
        foreign_relay(beside).wait_send()

    def outer_role(level):
        beside, other, opp = NEIGHBOUR[level], 3 - level, (level + 2) % LEVELS
        arrived.clear()
        wait_weights()
        w_copy(level, 3, beside).start()
        for k in order:
            wait_own(k)
            to_inner(k, beside).start()
        w_copy(beside, 3, beside).wait_recv()
        w_copy(opp, 6, beside).wait_recv()
        w_copy(other, 7, beside).wait_recv()
        for k in order:
            if sends_own(beside, k):
                outward_q(k, 0, beside).wait_recv()
            outward_relay(k, beside).wait_recv()
            if sends_opposite(beside, k):
                outward_q(k, 1, beside).wait_recv()
            finish(k, level)
            if k == order[-1]:
                foreign_relay(beside).wait_recv()
                acc[0] += fore_in[0]
                for o in (1, 2, 3):
                    share(o).start()
            send_back(k)
        for k in order:
            to_inner(k, beside).wait_send()
        w_copy(level, 3, beside).wait_send()

    for level in range(LEVELS):
        role = inner_role if level in (1, 2) else outer_role
        pl.when(z == level)(functools.partial(role, level))

    average = pltpu.make_async_copy(avgbuf.at[z], avg_ref, avg_sem)
    average.start()

    for o in (1, 2, 3):
        share(o).wait_recv()
    spread_part[...] = acc[0, r] + spread_in[0] + spread_in[1] + spread_in[2]
    swap = remote(spread_part, spread_x, s_send.at[3], s_recv.at[3], {"blk": 1 - side})
    swap.start()
    for k in range(chunks):
        for o in (1, 2, 3):
            near(k, o).wait_send()
            back(k, o).wait()
        back_local(k).wait()
    for o in (1, 2, 3):
        w_near(o).wait_send()
        share(o).wait_send()
    average.wait()
    swap.wait()
    spread_ref[0] = jnp.sum(spread_part[...] + spread_x[...]) / (row_total * hidden)


def fused(params, weights):
    _, rows, hidden = params.shape
    node_count = lax.axis_size("node")
    width = hidden // node_count
    piece = rows // SPLIT
    chunks = LEVELS * SPLIT
    raw = pltpu.VMEM((chunks, GROUP, piece, width), params.dtype)
    q = pltpu.VMEM((chunks, piece, width), jnp.float32)
    tile = pltpu.VMEM((8, LANES), jnp.float32)
    dma = pltpu.SemaphoreType.DMA
    debiased, average, spread = pl.pallas_call(
        kernel,
        out_shape=(
            jax.ShapeDtypeStruct((1, rows, hidden), jnp.float32),
            jax.ShapeDtypeStruct((rows, width), jnp.float32),
            jax.ShapeDtypeStruct((1,), jnp.float32),
        ),
        in_specs=[pl.BlockSpec(memory_space=pltpu.HBM), pl.BlockSpec(memory_space=pltpu.SMEM)],
        out_specs=(pl.BlockSpec(memory_space=pl.ANY), pl.BlockSpec(memory_space=pl.ANY),
                   pl.BlockSpec(memory_space=pltpu.SMEM)),
        scratch_shapes=[
            raw, raw, raw, raw, q, q,
            pltpu.VMEM((chunks, 2, piece, width), jnp.float32),
            pltpu.VMEM((chunks, GROUP, piece, width), jnp.float32),
            pltpu.VMEM((LEVELS, rows, width), jnp.float32),
            pltpu.VMEM((LEVELS, GROUP, 8, LANES), jnp.float32),
            pltpu.VMEM((3, GROUP, 8, LANES), jnp.float32),
            pltpu.VMEM((3, 8, LANES), jnp.float32),
            tile, tile,
            dma((chunks, 3)), dma((chunks, 3)), dma((chunks,)),
            dma((chunks, 5)), dma((chunks, 5)),
            dma((chunks, 3)), dma((chunks, 3)), dma((chunks,)),
            dma((8,)), dma((8,)), dma((4,)), dma((4,)), dma,
            pltpu.VMEM((2, GROUP, 8, LANES), jnp.float32), dma((2,)), dma((2,)),
        ],
        compiler_params=pltpu.CompilerParams(
            collective_id=0, has_side_effects=True, vmem_limit_bytes=20 << 20),
    )(params, weights)
    return debiased, average, spread


def from_behind(value, axis, steps):
    count = lax.axis_size(axis)
    pairs = [(source, (source + steps) % count) for source in range(count)]
    return lax.ppermute(value, axis, pairs)


def push_round(value, scale, hop):
    received = from_behind((value, scale), "node", hop)
    return (received[0], received[1])


def shards(params, weights):
    node_count = lax.axis_size("node")
    levels = node_count.bit_length() - 1
    scale0 = weights.astype(jnp.float32)
    weighted = scale0[:, None, None] * params.astype(jnp.float32)
    value = weighted
    scale = scale0
    for step in range(ROUNDS):
        hop = 1 << step % levels
        if step == 0:
            raw = from_behind((params, weights.astype(jnp.bfloat16)), "node", hop)
            other_scale = raw[1].astype(jnp.float32)
            other_value = other_scale[:, None, None] * raw[0].astype(jnp.float32)
        else:
            other_value, other_scale = push_round(value, scale, hop)
        value = 0.5 * value + 0.5 * other_value
        scale = 0.5 * scale + 0.5 * other_scale
    debiased = value / scale[:, None, None]
    hidden_units = params.shape[2]
    width = hidden_units // node_count
    local = debiased[0]
    numer, total = lax.psum((weighted[0], jnp.sum(scale0)), "node")
    whole = numer / total
    partial_value = jnp.sum((local - whole) ** 2)[None]
    average = lax.dynamic_slice_in_dim(whole, lax.axis_index("node") * width, width, 1)
    row_count = params.shape[1] * lax.axis_size("blk")
    spread = lax.psum(partial_value, "blk") / (row_count * hidden_units)
    return (debiased, average, spread)


def solution(mesh):
    line = mesh.shape["node"] == GROUP * LEVELS and mesh.shape["blk"] == 2
    return jax.shard_map(
        fused if line else shards,
        mesh=mesh,
        in_specs=(P("node", "blk", None), P("node")),
        out_specs=(P("node", "blk", None), P("blk", "node"), P("node")),
        check_vma=False,
    )
```

profile of v0, /device:TPU:0, one launch (start us, length us, event | category | flops | bytes accessed | tf_op | source)
XLA Modules:
  0.0 106.9 jit_solution(11567871588676447809)
XLA Ops:
  1.3 0.0 copy-start
  1.3 1.5 %copy-done = bf16[1,64,14336]{2,1,0:T(8,128)(2,1)S(1)} copy-done((bf16[1,64,14336]{2,1,0:T(8,128)(2,1)S(1)}, bf16[1,64,14336]{2,1,0:T(8,128)(2,1)}, u32[]{:S(2)}) %copy-start) | copy-done | bytes 1835032
  2.8 99.8 %shard_map.49 = (f32[1,64,14336]{2,1,0:T(8,128)S(1)}, f32[64,896]{1,0:T(8,128)S(1)}, f32[1]{0:T(128)}) custom-call(bf16[1,64,14336]{2,1,0:T(8,128)(2,1)S(1)} %copy-done, s32[1]{0:T(128)S(6)} %copy.8.w_ref), custom_call_target="tpu_custom_call" | custom-call | tf_op jit(solution)/shard_map/pallas_call | solution.py:410
  102.6 1.8 %copy.9 = f32[1,64,14336]{2,1,0:T(8,128)} copy(f32[1,64,14336]{2,1,0:T(8,128)S(1)} %get-tuple-element.6) | data formatting | bytes 7340032
  104.4 0.7 copy.10
Async XLA Ops:
  1.3 1.5 %copy-start = (bf16[1,64,14336]{2,1,0:T(8,128)(2,1)S(1)}, bf16[1,64,14336]{2,1,0:T(8,128)(2,1)}, u32[]{:S(2)}) copy-start(bf16[1,64,14336]{2,1,0:T(8,128)(2,1)} %p_ref.1) | copy-start | bytes 5505028
where the time goes:
time: 107 us
  Pallas kernels  99.8 us (93%)
  local copies, waits for them, and re-layouts  4.02 us (4%)
  between operations  3.06 us (3%)
    pallas_call x1, Pallas kernels, fused(): pl.pallas_call(kernel, out_shape=(jax.ShapeDtypeStruct((1, rows, hidden),...  99.8 us
    unnamed x4, local copies, waits for them, and re-layouts  4.02 us

commit v1 on v0

v1 whole, which is shorter than its diff:
```python
import functools

import jax
import jax.numpy as jnp
from jax import lax
from jax.experimental import pallas as pl
from jax.experimental.pallas import tpu as pltpu
from jax.sharding import PartitionSpec as P

ROUNDS = 3
GROUP = 4
LEVELS = 4
SPLIT = 4
LANES = 128
AHEAD = 4
NEIGHBOUR = (1, 0, 3, 2)


def kernel(p_ref, w_ref, out_ref, avg_ref, spread_ref,
           raw_own, raw_a, raw_b, raw_c, q_in, q_out, dbuf, avgbuf,
           wts, acc, part, spread_in,
           near_send, near_recv, own_sem, back_send, back_recv, back_own,
           piece_send, piece_recv, far_send, far_recv,
           w_send, w_recv, s_send, s_recv, avg_send, avg_recv):
    node = lax.axis_index("node")
    side = lax.axis_index("blk")
    z = node // GROUP
    r = node % GROUP
    half, core = r // 2, r % 2
    chunks, _, rows, width = raw_own.shape
    hidden = p_ref.shape[2]
    row_total = p_ref.shape[1] * lax.axis_size("blk")
    middle = chunks // 2

    lows = list(range(middle))
    highs = list(range(middle + SPLIT, chunks)) + list(range(middle, middle + SPLIT))
    order = [k for pair in zip(lows, highs) for k in pair]
    first = order[:AHEAD]

    def peer(o):
        y = 1 - half if o & 2 else half
        c = 1 - core if o & 1 else core
        return y * 2 + c

    def dev(zz, rr):
        return {"node": zz * GROUP + rr}

    inner = jnp.logical_and(z >= 1, z <= 2)
    mate = 3 - z
    nb = (z // 2) * 2 + 1 - z % 2
    inner_count = (1 - z // 3) * ((z + 2) // 3)

    def remote(src, dst, ssem, rsem, device):
        return pltpu.make_async_remote_copy(
            src_ref=src, dst_ref=dst, send_sem=ssem, recv_sem=rsem,
            device_id=device, device_id_type=pl.DeviceIdType.MESH)

    def own_slice(k):
        return pl.ds((k % SPLIT) * rows, rows)

    def block(k, rr):
        return pl.ds(pl.multiple_of(((k // SPLIT) * GROUP + rr) * width, LANES), width)

    barrier = pltpu.get_barrier_semaphore()

    def greet(device):
        pl.semaphore_signal(barrier, inc=1, device_id=device,
                            device_id_type=pl.DeviceIdType.MESH)

    for o in (1, 2, 3):
        greet(dev(z, peer(o)))
    greet({"blk": 1 - side})
    greet(dev(nb, r))

    @pl.when(inner)
    def _():
        greet(dev(mate, r))

    def local_in(k):
        return pltpu.make_async_copy(
            p_ref.at[0, own_slice(k), block(k, r)], raw_own.at[k, r], own_sem.at[k])

    for k in order:
        local_in(k).start()
    wts[z, r] = jnp.full((8, LANES), w_ref[0].astype(jnp.float32))
    acc[...] = jnp.zeros_like(acc)

    pl.semaphore_wait(barrier, 5 + inner_count)

    def w_near(o):
        return remote(wts.at[z, r], wts.at[z, r], w_send.at[o - 1], w_recv.at[o - 1],
                      dev(z, peer(o)))

    def near(k, o):
        return remote(p_ref.at[0, own_slice(k), block(k, peer(o))], raw_own.at[k, r],
                      near_send.at[k, o - 1], near_recv.at[k, o - 1], dev(z, peer(o)))

    def send_near(ks):
        for k in ks:
            for o in (2, 3, 1):
                near(k, o).start()

    arrived = set()

    def wait_piece(k, o):
        if (k, o) in arrived:
            return
        arrived.add((k, o))
        if o:
            near(k, o).wait_recv()
        else:
            local_in(k).wait()

    def wait_own(k):
        for o in range(GROUP):
            wait_piece(k, o)

    def row(zz, i):
        return wts[zz, i, 0:1, :]

    def value(ref, k, zz, i, cols):
        return ref[k, i, :, cols].astype(jnp.float32) * row(zz, i)

    def group_sum(ref, k, zz, cols):
        return ((value(ref, k, zz, 0, cols) + value(ref, k, zz, 1, cols))
                + (value(ref, k, zz, 2, cols) + value(ref, k, zz, 3, cols)))

    def columns(j):
        return pl.ds(pl.multiple_of(j * LANES, LANES), LANES)

    def back(k, o):
        return remote(dbuf.at[k, peer(o)], out_ref.at[0, own_slice(k), block(k, r)],
                      back_send.at[k, o - 1], back_recv.at[k, o - 1], dev(z, peer(o)))

    def back_local(k):
        return pltpu.make_async_copy(
            dbuf.at[k, r], out_ref.at[0, own_slice(k), block(k, r)], back_own.at[k])

    def send_back(k):
        for o in (2, 3, 1):
            back(k, o).start()
        back_local(k).start()

    def group_weight(zz):
        return row(zz, 0) + row(zz, 1) + row(zz, 2) + row(zz, 3)

    def scales_of(level):
        opp = (level + 2) % LEVELS
        sums = [group_weight((level + 3) % LEVELS)] * GROUP
        for i in range(GROUP):
            for e in range(GROUP):
                sums[i] = sums[i] + row(level if e <= i else opp, e)
        return [1.0 / total for total in sums]

    def window(own, tail, prior):
        heads = [own[0]]
        for i in range(1, GROUP):
            heads.append(heads[-1] + own[i])
        tails = [None, None, None, tail[3]]
        for i in (2, 1):
            tails[i] = tails[i + 1] + tail[i]
        sums = [head + prior for head in heads]
        return [sums[i] + tails[i + 1] for i in range(GROUP - 1)] + [sums[-1]]

    def debias(k, level, prior_ref, tail_ref):
        opp, prior_level = (level + 2) % LEVELS, (level + 3) % LEVELS
        scales = scales_of(level)

        def step(j, carry):
            cols = columns(j)
            if prior_ref is None:
                prior = q_in[k, :, cols]
            else:
                prior = group_sum(prior_ref, k, prior_level, cols)
            own = [value(raw_own, k, level, i, cols) for i in range(GROUP)]
            tail = [None] + [value(tail_ref, k, opp, i, cols) for i in range(1, GROUP)]
            for i, total in enumerate(window(own, tail, prior)):
                dbuf[k, i, :, cols] = total * scales[i]
            return carry

        lax.fori_loop(0, width // LANES, step, 0)

    def means(k, level):
        refs = {level: raw_own, NEIGHBOUR[level]: raw_a, 3 - level: raw_b,
                (level + 2) % LEVELS: raw_c}
        slot = 1 if k // SPLIT == level else 0
        whole = 1.0 / (group_weight(0) + group_weight(1) + group_weight(2) + group_weight(3))
        scales = [scales_of(y) for y in range(LEVELS)]

        def step(j, sums):
            cols = columns(j)
            groups = [group_sum(refs[y], k, y, cols) for y in range(LEVELS)]
            mean = ((groups[0] + groups[1]) + (groups[2] + groups[3])) * whole
            avgbuf[slot, own_slice(k), cols] = mean
            fresh = []
            for y in range(LEVELS):
                far = (y + 2) % LEVELS
                own = [value(refs[y], k, y, i, cols) for i in range(GROUP)]
                tail = [None] + [value(refs[far], k, far, i, cols) for i in range(1, GROUP)]
                for i, total in enumerate(window(own, tail, groups[(y + 3) % LEVELS])):
                    gap = total * scales[y][i] - mean
                    gap = gap * gap
                    fold = gap[0:8]
                    for e in range(8, rows, 8):
                        fold = fold + gap[e:e + 8]
                    fresh.append(sums[y * GROUP + i] + fold)
            return tuple(fresh)

        zero = jnp.zeros((8, LANES), jnp.float32)
        sums = lax.fori_loop(0, width // LANES, step, (zero,) * (LEVELS * GROUP))
        for y in range(LEVELS):
            for i in range(GROUP):
                acc[y, i] += sums[y * GROUP + i]

    def nodes(full):
        return pl.ds(0, GROUP) if full else pl.ds(1, GROUP - 1)

    def to_inner(k, beside):
        return remote(raw_own.at[k], raw_a.at[k], far_send.at[k, 0], far_recv.at[k, 0],
                      dev(beside, r))

    def piece(k, o, source):
        n = first.index(k)
        return remote(raw_own.at[k, peer(o)], raw_b.at[k, peer(o)], piece_send.at[n, o],
                      piece_recv.at[n, o], dev(3 - source, r))

    def with_piece(k, o, source, act):
        if source == 1 or k < middle:
            act()
        else:
            pl.when(peer(o) != 0)(act)

    def across(k, source):
        part_of = nodes(source == 1)
        return remote(raw_own.at[k, part_of], raw_b.at[k, part_of], far_send.at[k, 0],
                      far_recv.at[k, 1], dev(3 - source, r))

    def across_wait(k, source, sent):
        if k not in first:
            copy = across(k, source)
            copy.wait_send() if sent else copy.wait_recv()
            return
        for o in range(GROUP):
            copy = piece(k, o, source)
            with_piece(k, o, source, copy.wait_send if sent else copy.wait_recv)

    def across_relay(k, source):
        part_of = nodes(source == 2)
        return remote(raw_a.at[k, part_of], raw_c.at[k, part_of], far_send.at[k, 1],
                      far_recv.at[k, 2], dev(3 - source, r))

    def extra(k, source):
        n = k % middle
        if source == 1:
            src, dst = raw_a, raw_c
        else:
            src, dst = raw_own, raw_b
        return remote(src.at[k, 0], dst.at[k, 0], far_send.at[n, 4], far_recv.at[n, 4],
                      dev(3 - source, r))

    def outward_relay(k, source):
        part_of = nodes(False)
        return remote(raw_b.at[k, part_of], raw_a.at[k, part_of], far_send.at[k, 2],
                      far_recv.at[k, 0], dev(NEIGHBOUR[source], r))

    def outward_q(k, source):
        return remote(q_out.at[k], q_in.at[k], far_send.at[k, 3], far_recv.at[k, 3],
                      dev(NEIGHBOUR[source], r))

    def outward_mean(k, source):
        n = k % SPLIT
        return remote(avgbuf.at[0, own_slice(k)], avg_ref.at[own_slice(k)],
                      avg_send.at[n], avg_recv.at[n], dev(NEIGHBOUR[source], r))

    def own_mean(k):
        n = k % SPLIT
        return pltpu.make_async_copy(
            avgbuf.at[1, own_slice(k)], avg_ref.at[own_slice(k)], avg_recv.at[n])

    def w_copy(level, slot, target):
        return remote(wts.at[level], wts.at[level], w_send.at[slot], w_recv.at[slot],
                      dev(target, r))

    def spread_slot(level, x, rr):
        return (level - 1) * 2 * GROUP + x * GROUP + rr

    def share(level, y, o, flip):
        x = 1 - side if flip else side
        return remote(part.at[y, peer(o)], spread_in.at[spread_slot(level, side, r)],
                      s_send.at[y, o, flip], s_recv.at[spread_slot(level, side, r)],
                      {"node": y * GROUP + peer(o), "blk": x})

    def shares(level):
        return [(y, o, flip) for y in (3 - level, (level + 2) % LEVELS, NEIGHBOUR[level], level)
                for flip in (1, 0) for o in (3, 2, 1, 0) if y != level or flip or o]

    def gather_spread(level):
        for maker in (1, 2):
            for flip in (0, 1):
                x = 1 - side if flip else side
                for o in range(GROUP):
                    if maker == level and not flip and not o:
                        continue
                    slot = spread_slot(maker, x, peer(o))
                    remote(part.at[0, 0], spread_in.at[slot], s_send.at[0, 0, 0],
                           s_recv.at[slot], {"blk": 1 - side}).wait_recv()

    def inner_role(level):
        beside, other, opp = NEIGHBOUR[level], 3 - level, (level + 2) % LEVELS
        arrived.clear()
        sent_extras = [k for k in (highs if level == 1 else lows)
                       if level == 1 or k not in first]
        mine = lows if level == 1 else highs
        prior_ref = raw_a if level == 1 else raw_b

        def make_q(k):
            src, zz = (raw_c, opp) if level == 1 else (raw_own, level)

            def step(j, carry):
                cols = columns(j)
                q_out[k, :, cols] = group_sum(src, k, zz, cols)
                return carry

            lax.fori_loop(0, width // LANES, step, 0)
            outward_q(k, level).start()

        for k in first:
            wait_piece(k, 0)
            with_piece(k, 0, level, piece(k, 0, level).start)
        send_near(first)
        for o in (1, 2, 3):
            w_near(o).start()
        send_near(order[AHEAD:])
        for k in first:
            wait_piece(k, 1)
            with_piece(k, 1, level, piece(k, 1, level).start)
        for n, k in enumerate(first):
            for o in (2, 3):
                wait_piece(k, o)
                with_piece(k, o, level, piece(k, o, level).start)
            if n == 0:
                for o in (1, 2, 3):
                    w_near(o).wait_recv()
                w_copy(level, 3, beside).start()
                w_copy(level, 4, other).start()

        for t in range(chunks + 2):
            if t + AHEAD < chunks:
                wait_own(order[t + AHEAD])
                across(order[t + AHEAD], level).start()
            if t < chunks:
                k = order[t]
                to_inner(k, beside).wait_recv()
                across_relay(k, level).start()
                if t == 0:
                    w_copy(beside, 3, beside).wait_recv()
                    w_copy(beside, 5, other).start()
                    w_copy(level, 4, other).wait_recv()
                    w_copy(other, 6, beside).start()
                if t == chunks - 1:
                    for e in sent_extras:
                        extra(e, level).start()
                if level == 2:
                    make_q(k)
                across_wait(k, other, False)
                outward_relay(k, level).start()
            if t == 2:
                w_copy(opp, 5, other).wait_recv()
                w_copy(opp, 7, beside).start()
            if t >= 2:
                k = order[t - 2]
                across_relay(k, other).wait_recv()
                if level == 1:
                    make_q(k)
                debias(k, level, prior_ref, raw_c)
                send_back(k)
        for k in mine:
            if level == 2 or k not in first:
                extra(k, other).wait_recv()
            means(k, level)
            if k // SPLIT == level:
                own_mean(k).start()
            else:
                outward_mean(k, level).start()
        for y in range(LEVELS):
            for i in range(GROUP):
                part[y, i] = jnp.sum(acc[y, i], axis=0, keepdims=True)
        for y, o, flip in shares(level):
            share(level, y, o, flip).start()
        spread_in[spread_slot(level, side, r)] = part[level, r]

        for k in order:
            across_wait(k, level, True)
            across_relay(k, level).wait_send()
            outward_relay(k, level).wait_send()
            outward_q(k, level).wait_send()
        for k in sent_extras:
            extra(k, level).wait_send()
        w_copy(level, 3, beside).wait_send()
        w_copy(level, 4, other).wait_send()
        w_copy(beside, 5, other).wait_send()
        w_copy(other, 6, beside).wait_send()
        w_copy(opp, 7, beside).wait_send()
        for k in mine:
            if k // SPLIT == level:
                own_mean(k).wait()
            else:
                outward_mean(k, level).wait_send()
        gather_spread(level)
        for y, o, flip in shares(level):
            share(level, y, o, flip).wait_send()

    def outer_role(level):
        beside, other, opp = NEIGHBOUR[level], 3 - level, (level + 2) % LEVELS
        arrived.clear()
        send_near(first)
        for o in (1, 2, 3):
            w_near(o).start()
        send_near(order[AHEAD:])
        for n, k in enumerate(order):
            wait_own(k)
            to_inner(k, beside).start()
            if n == 0:
                for o in (1, 2, 3):
                    w_near(o).wait_recv()
                w_copy(level, 3, beside).start()
        w_copy(beside, 3, beside).wait_recv()
        w_copy(opp, 6, beside).wait_recv()
        w_copy(other, 7, beside).wait_recv()
        for k in order:
            outward_relay(k, beside).wait_recv()
            outward_q(k, beside).wait_recv()
            debias(k, level, None, raw_a)
            send_back(k)
        for k in order:
            to_inner(k, beside).wait_send()
        w_copy(level, 3, beside).wait_send()
        for k in range(SPLIT):
            outward_mean(k + level * SPLIT, beside).wait_recv()
        gather_spread(level)

    for level in range(LEVELS):
        role = inner_role if level in (1, 2) else outer_role
        pl.when(z == level)(functools.partial(role, level))

    for k in order:
        for o in (1, 2, 3):
            near(k, o).wait_send()
            back(k, o).wait()
        back_local(k).wait()
    for o in (1, 2, 3):
        w_near(o).wait_send()
    total = spread_in[0]
    for slot in range(1, spread_in.shape[0]):
        total = total + spread_in[slot]
    spread_ref[0] = jnp.sum(total) / (row_total * hidden)


def fused(params, weights):
    _, rows, hidden = params.shape
    node_count = lax.axis_size("node")
    width = hidden // node_count
    piece_rows = rows // SPLIT
    chunks = LEVELS * SPLIT
    raw = pltpu.VMEM((chunks, GROUP, piece_rows, width), params.dtype)
    q = pltpu.VMEM((chunks, piece_rows, width), jnp.float32)
    dma = pltpu.SemaphoreType.DMA
    debiased, average, spread = pl.pallas_call(
        kernel,
        out_shape=(
            jax.ShapeDtypeStruct((1, rows, hidden), jnp.float32),
            jax.ShapeDtypeStruct((rows, width), jnp.float32),
            jax.ShapeDtypeStruct((1,), jnp.float32),
        ),
        in_specs=[pl.BlockSpec(memory_space=pltpu.HBM), pl.BlockSpec(memory_space=pltpu.SMEM)],
        out_specs=(pl.BlockSpec(memory_space=pl.ANY), pl.BlockSpec(memory_space=pl.ANY),
                   pl.BlockSpec(memory_space=pltpu.SMEM)),
        scratch_shapes=[
            raw, raw, raw, raw, q, q,
            pltpu.VMEM((chunks, GROUP, piece_rows, width), jnp.float32),
            pltpu.VMEM((2, rows, width), jnp.float32),
            pltpu.VMEM((LEVELS, GROUP, 8, LANES), jnp.float32),
            pltpu.VMEM((LEVELS, GROUP, 8, LANES), jnp.float32),
            pltpu.VMEM((LEVELS, GROUP, 1, LANES), jnp.float32),
            pltpu.VMEM((4 * GROUP, 1, LANES), jnp.float32),
            dma((chunks, 3)), dma((chunks, 3)), dma((chunks,)),
            dma((chunks, 3)), dma((chunks, 3)), dma((chunks,)),
            dma((AHEAD, GROUP)), dma((AHEAD, GROUP)),
            dma((chunks, 5)), dma((chunks, 5)),
            dma((8,)), dma((8,)), dma((LEVELS, GROUP, 2)), dma((4 * GROUP,)),
            dma((SPLIT,)), dma((SPLIT,)),
        ],
        compiler_params=pltpu.CompilerParams(
            collective_id=0, has_side_effects=True, vmem_limit_bytes=20 << 20),
    )(params, weights)
    return debiased, average, spread


def from_behind(value, axis, steps):
    count = lax.axis_size(axis)
    pairs = [(source, (source + steps) % count) for source in range(count)]
    return lax.ppermute(value, axis, pairs)


def push_round(value, scale, hop):
    received = from_behind((value, scale), "node", hop)
    return (received[0], received[1])


def shards(params, weights):
    node_count = lax.axis_size("node")
    levels = node_count.bit_length() - 1
    scale0 = weights.astype(jnp.float32)
    weighted = scale0[:, None, None] * params.astype(jnp.float32)
    value = weighted
    scale = scale0
    for step in range(ROUNDS):
        hop = 1 << step % levels
        if step == 0:
            raw = from_behind((params, weights.astype(jnp.bfloat16)), "node", hop)
            other_scale = raw[1].astype(jnp.float32)
            other_value = other_scale[:, None, None] * raw[0].astype(jnp.float32)
        else:
            other_value, other_scale = push_round(value, scale, hop)
        value = 0.5 * value + 0.5 * other_value
        scale = 0.5 * scale + 0.5 * other_scale
    debiased = value / scale[:, None, None]
    hidden_units = params.shape[2]
    width = hidden_units // node_count
    local = debiased[0]
    numer, total = lax.psum((weighted[0], jnp.sum(scale0)), "node")
    whole = numer / total
    partial_value = jnp.sum((local - whole) ** 2)[None]
    average = lax.dynamic_slice_in_dim(whole, lax.axis_index("node") * width, width, 1)
    row_count = params.shape[1] * lax.axis_size("blk")
    spread = lax.psum(partial_value, "blk") / (row_count * hidden_units)
    return (debiased, average, spread)


def solution(mesh):
    line = mesh.shape["node"] == GROUP * LEVELS and mesh.shape["blk"] == 2
    return jax.shard_map(
        fused if line else shards,
        mesh=mesh,
        in_specs=(P("node", "blk", None), P("node")),
        out_specs=(P("node", "blk", None), P("blk", "node"), P("node")),
        check_vma=False,
    )
```

time: 107 us -> 101 us (0.944)
  Pallas kernels: 99.8 us -> 94.2 us
    pallas_call x1, Pallas kernels: 99.8 us -> 94.2 us  [fused(): pl.pallas_call(kernel, out_shape=(jax.ShapeDtypeStruct((1, rows, hidden),...]
where the time goes in v1:
time: 101 us
  Pallas kernels  94.2 us (93%)
  local copies, waits for them, and re-layouts  4.02 us (4%)
  between operations  3.06 us (3%)
    pallas_call x1, Pallas kernels, fused(): pl.pallas_call(kernel, out_shape=(jax.ShapeDtypeStruct((1, rows, hidden),...  94.2 us
    unnamed x4, local copies, waits for them, and re-layouts  4.02 us

profile of v1, /device:TPU:0, one launch (start us, length us, event | category | flops | bytes accessed | tf_op | source)
XLA Modules:
  0.0 101.3 jit_solution(5141243341306514239)
XLA Ops:
  1.3 0.0 copy-start
  1.3 1.5 %copy-done = bf16[1,64,14336]{2,1,0:T(8,128)(2,1)S(1)} copy-done((bf16[1,64,14336]{2,1,0:T(8,128)(2,1)S(1)}, bf16[1,64,14336]{2,1,0:T(8,128)(2,1)}, u32[]{:S(2)}) %copy-start) | copy-done | bytes 1835032
  2.8 94.2 %shard_map.49 = (f32[1,64,14336]{2,1,0:T(8,128)S(1)}, f32[64,896]{1,0:T(8,128)S(1)}, f32[1]{0:T(128)}) custom-call(bf16[1,64,14336]{2,1,0:T(8,128)(2,1)S(1)} %copy-done, s32[1]{0:T(128)S(6)} %copy.8.w_ref), custom_call_target="tpu_custom_call" | custom-call | tf_op jit(solution)/shard_map/pallas_call | solution.py:468
  97.0 1.8 %copy.9 = f32[1,64,14336]{2,1,0:T(8,128)} copy(f32[1,64,14336]{2,1,0:T(8,128)S(1)} %get-tuple-element.6) | data formatting | bytes 7340032
  98.8 0.7 copy.10
Async XLA Ops:
  1.3 1.5 %copy-start = (bf16[1,64,14336]{2,1,0:T(8,128)(2,1)S(1)}, bf16[1,64,14336]{2,1,0:T(8,128)(2,1)}, u32[]{:S(2)}) copy-start(bf16[1,64,14336]{2,1,0:T(8,128)(2,1)} %p_ref.1) | copy-start | bytes 5505028

commit v2 on v1

--- a/solution.py
+++ b/solution.py
@@ -12,15 +12,16 @@
 LEVELS = 4
 SPLIT = 4
 LANES = 128
-AHEAD = 4
+AHEAD = 2
+LATE = 4
 NEIGHBOUR = (1, 0, 3, 2)
 
 
 def kernel(p_ref, w_ref, out_ref, avg_ref, spread_ref,
            raw_own, raw_a, raw_b, raw_c, q_in, q_out, dbuf, avgbuf,
            wts, acc, part, spread_in,
-           near_send, near_recv, own_sem, back_send, back_recv, back_own,
-           piece_send, piece_recv, far_send, far_recv,
+           near_send, near_recv, beside_recv, own_sem, back_send, back_recv, back_own,
+           far_send, own_recv, relay_recv, beside_in, q_recv, extra_recv,
            w_send, w_recv, s_send, s_recv, avg_send, avg_recv):
     node = lax.axis_index("node")
     side = lax.axis_index("blk")
@@ -55,6 +56,9 @@
             src_ref=src, dst_ref=dst, send_sem=ssem, recv_sem=rsem,
             device_id=device, device_id_type=pl.DeviceIdType.MESH)
 
+    def drain(ref, sem):
+        pltpu.make_async_copy(ref, ref, sem).wait()
+
     def own_slice(k):
         return pl.ds((k % SPLIT) * rows, rows)
 
@@ -78,7 +82,7 @@
 
     def local_in(k):
         return pltpu.make_async_copy(
-            p_ref.at[0, own_slice(k), block(k, r)], raw_own.at[k, r], own_sem.at[k])
+            p_ref.at[0, own_slice(k), block(k, r)], raw_own.at[k, r], own_sem)
 
     for k in order:
         local_in(k).start()
@@ -86,34 +90,31 @@
     acc[...] = jnp.zeros_like(acc)
 
     pl.semaphore_wait(barrier, 5 + inner_count)
+    drain(raw_own.at[:, 0], own_sem)
 
     def w_near(o):
-        return remote(wts.at[z, r], wts.at[z, r], w_send.at[o - 1], w_recv.at[o - 1],
+        return remote(wts.at[z, r], wts.at[z, r], w_send.at[0], w_recv.at[0],
                       dev(z, peer(o)))
 
     def near(k, o):
         return remote(p_ref.at[0, own_slice(k), block(k, peer(o))], raw_own.at[k, r],
-                      near_send.at[k, o - 1], near_recv.at[k, o - 1], dev(z, peer(o)))
+                      near_send, beside_recv.at[first.index(k)] if k in first and o == 1
+                      else near_recv.at[k], dev(z, peer(o)))
 
     def send_near(ks):
         for k in ks:
             for o in (2, 3, 1):
                 near(k, o).start()
 
-    arrived = set()
-
-    def wait_piece(k, o):
-        if (k, o) in arrived:
-            return
-        arrived.add((k, o))
-        if o:
-            near(k, o).wait_recv()
-        else:
-            local_in(k).wait()
-
-    def wait_own(k):
-        for o in range(GROUP):
-            wait_piece(k, o)
+    def near_weights():
+        drain(wts.at[0, pl.ds(0, GROUP - 1)], w_recv.at[0])
+
+    def wait_beside(k):
+        drain(raw_own.at[k, 0], beside_recv.at[first.index(k)])
+
+    def wait_near(k):
+        count = GROUP - 2 if k in first else GROUP - 1
+        drain(raw_own.at[k, pl.ds(0, count)], near_recv.at[k])
 
     def row(zz, i):
         return wts[zz, i, 0:1, :]
@@ -130,11 +131,11 @@
 
     def back(k, o):
         return remote(dbuf.at[k, peer(o)], out_ref.at[0, own_slice(k), block(k, r)],
-                      back_send.at[k, o - 1], back_recv.at[k, o - 1], dev(z, peer(o)))
+                      back_send, back_recv, dev(z, peer(o)))
 
     def back_local(k):
         return pltpu.make_async_copy(
-            dbuf.at[k, r], out_ref.at[0, own_slice(k), block(k, r)], back_own.at[k])
+            dbuf.at[k, r], out_ref.at[0, own_slice(k), block(k, r)], back_own)
 
     def send_back(k):
         for o in (2, 3, 1):
@@ -216,66 +217,69 @@
         return pl.ds(0, GROUP) if full else pl.ds(1, GROUP - 1)
 
     def to_inner(k, beside):
-        return remote(raw_own.at[k], raw_a.at[k], far_send.at[k, 0], far_recv.at[k, 0],
+        return remote(raw_own.at[k], raw_a.at[k], far_send.at[0], beside_in.at[k],
                       dev(beside, r))
 
     def piece(k, o, source):
-        n = first.index(k)
-        return remote(raw_own.at[k, peer(o)], raw_b.at[k, peer(o)], piece_send.at[n, o],
-                      piece_recv.at[n, o], dev(3 - source, r))
-
-    def with_piece(k, o, source, act):
-        if source == 1 or k < middle:
-            act()
+        return remote(raw_own.at[k, peer(o)], raw_b.at[k, peer(o)],
+                      far_send.at[6 if all_own(k, source) else 7], own_recv.at[k],
+                      dev(3 - source, r))
+
+    def all_own(k, source):
+        return source == 1 or (k in first and k < middle)
+
+    def send_piece(k, o, source):
+        start = piece(k, o, source).start
+        if all_own(k, source):
+            start()
         else:
-            pl.when(peer(o) != 0)(act)
+            pl.when(peer(o) != 0)(start)
 
     def across(k, source):
         part_of = nodes(source == 1)
-        return remote(raw_own.at[k, part_of], raw_b.at[k, part_of], far_send.at[k, 0],
-                      far_recv.at[k, 1], dev(3 - source, r))
-
-    def across_wait(k, source, sent):
-        if k not in first:
-            copy = across(k, source)
-            copy.wait_send() if sent else copy.wait_recv()
-            return
-        for o in range(GROUP):
-            copy = piece(k, o, source)
-            with_piece(k, o, source, copy.wait_send if sent else copy.wait_recv)
+        return remote(raw_own.at[k, part_of], raw_b.at[k, part_of], far_send.at[1],
+                      own_recv.at[k], dev(3 - source, r))
+
+    def across_wait(k, source):
+        drain(raw_b.at[k, nodes(all_own(k, source))], own_recv.at[k])
+
+    def across_sent(source):
+        drain(raw_own.at[pl.ds(0, chunks - AHEAD), nodes(source == 1)], far_send.at[1])
+        if source == 1:
+            drain(raw_own.at[pl.ds(0, AHEAD)], far_send.at[6])
+        else:
+            drain(raw_own.at[pl.ds(0, AHEAD // 2)], far_send.at[6])
+            drain(raw_own.at[pl.ds(0, AHEAD // 2), nodes(False)], far_send.at[7])
 
     def across_relay(k, source):
         part_of = nodes(source == 2)
-        return remote(raw_a.at[k, part_of], raw_c.at[k, part_of], far_send.at[k, 1],
-                      far_recv.at[k, 2], dev(3 - source, r))
+        return remote(raw_a.at[k, part_of], raw_c.at[k, part_of], far_send.at[2],
+                      relay_recv.at[k], dev(3 - source, r))
 
     def extra(k, source):
-        n = k % middle
         if source == 1:
             src, dst = raw_a, raw_c
         else:
             src, dst = raw_own, raw_b
-        return remote(src.at[k, 0], dst.at[k, 0], far_send.at[n, 4], far_recv.at[n, 4],
+        return remote(src.at[k, 0], dst.at[k, 0], far_send.at[3], extra_recv.at[k % middle],
                       dev(3 - source, r))
 
     def outward_relay(k, source):
         part_of = nodes(False)
-        return remote(raw_b.at[k, part_of], raw_a.at[k, part_of], far_send.at[k, 2],
-                      far_recv.at[k, 0], dev(NEIGHBOUR[source], r))
+        return remote(raw_b.at[k, part_of], raw_a.at[k, part_of], far_send.at[4],
+                      beside_in.at[k], dev(NEIGHBOUR[source], r))
 
     def outward_q(k, source):
-        return remote(q_out.at[k], q_in.at[k], far_send.at[k, 3], far_recv.at[k, 3],
+        return remote(q_out.at[k], q_in.at[k], far_send.at[5], q_recv.at[k],
                       dev(NEIGHBOUR[source], r))
 
     def outward_mean(k, source):
-        n = k % SPLIT
         return remote(avgbuf.at[0, own_slice(k)], avg_ref.at[own_slice(k)],
-                      avg_send.at[n], avg_recv.at[n], dev(NEIGHBOUR[source], r))
+                      avg_send, avg_recv, dev(NEIGHBOUR[source], r))
 
     def own_mean(k):
-        n = k % SPLIT
         return pltpu.make_async_copy(
-            avgbuf.at[1, own_slice(k)], avg_ref.at[own_slice(k)], avg_recv.at[n])
+            avgbuf.at[1, own_slice(k)], avg_ref.at[own_slice(k)], avg_recv)
 
     def w_copy(level, slot, target):
         return remote(wts.at[level], wts.at[level], w_send.at[slot], w_recv.at[slot],
@@ -287,7 +291,7 @@
     def share(level, y, o, flip):
         x = 1 - side if flip else side
         return remote(part.at[y, peer(o)], spread_in.at[spread_slot(level, side, r)],
-                      s_send.at[y, o, flip], s_recv.at[spread_slot(level, side, r)],
+                      s_send.at[flip], s_recv,
                       {"node": y * GROUP + peer(o), "blk": x})
 
     def shares(level):
@@ -295,22 +299,16 @@
                 for flip in (1, 0) for o in (3, 2, 1, 0) if y != level or flip or o]
 
     def gather_spread(level):
-        for maker in (1, 2):
-            for flip in (0, 1):
-                x = 1 - side if flip else side
-                for o in range(GROUP):
-                    if maker == level and not flip and not o:
-                        continue
-                    slot = spread_slot(maker, x, peer(o))
-                    remote(part.at[0, 0], spread_in.at[slot], s_send.at[0, 0, 0],
-                           s_recv.at[slot], {"blk": 1 - side}).wait_recv()
+        slots = spread_in.shape[0]
+        drain(spread_in.at[pl.ds(0, slots - 1 if level in (1, 2) else slots)], s_recv)
 
     def inner_role(level):
         beside, other, opp = NEIGHBOUR[level], 3 - level, (level + 2) % LEVELS
-        arrived.clear()
         sent_extras = [k for k in (highs if level == 1 else lows)
                        if level == 1 or k not in first]
+        late_sent = sent_extras[-LATE:]
         mine = lows if level == 1 else highs
+        late_mine = mine[-LATE:]
         prior_ref = raw_a if level == 1 else raw_b
 
         def make_q(k):
@@ -324,45 +322,54 @@
             lax.fori_loop(0, width // LANES, step, 0)
             outward_q(k, level).start()
 
+        def make_mean(k):
+            if level == 2 or k not in first:
+                extra(k, other).wait_recv()
+            means(k, level)
+            if k // SPLIT == level:
+                own_mean(k).start()
+            else:
+                outward_mean(k, level).start()
+
         for k in first:
-            wait_piece(k, 0)
-            with_piece(k, 0, level, piece(k, 0, level).start)
+            send_piece(k, 0, level)
         send_near(first)
         for o in (1, 2, 3):
             w_near(o).start()
         send_near(order[AHEAD:])
         for k in first:
-            wait_piece(k, 1)
-            with_piece(k, 1, level, piece(k, 1, level).start)
+            wait_beside(k)
+            send_piece(k, 1, level)
         for n, k in enumerate(first):
+            wait_near(k)
             for o in (2, 3):
-                wait_piece(k, o)
-                with_piece(k, o, level, piece(k, o, level).start)
+                send_piece(k, o, level)
             if n == 0:
-                for o in (1, 2, 3):
-                    w_near(o).wait_recv()
+                near_weights()
                 w_copy(level, 3, beside).start()
                 w_copy(level, 4, other).start()
 
         for t in range(chunks + 2):
             if t + AHEAD < chunks:
-                wait_own(order[t + AHEAD])
+                wait_near(order[t + AHEAD])
                 across(order[t + AHEAD], level).start()
             if t < chunks:
                 k = order[t]
                 to_inner(k, beside).wait_recv()
                 across_relay(k, level).start()
+                if k in sent_extras and k not in late_sent:
+                    extra(k, level).start()
                 if t == 0:
                     w_copy(beside, 3, beside).wait_recv()
                     w_copy(beside, 5, other).start()
                     w_copy(level, 4, other).wait_recv()
                     w_copy(other, 6, beside).start()
                 if t == chunks - 1:
-                    for e in sent_extras:
+                    for e in late_sent:
                         extra(e, level).start()
                 if level == 2:
                     make_q(k)
-                across_wait(k, other, False)
+                across_wait(k, other)
                 outward_relay(k, level).start()
             if t == 2:
                 w_copy(opp, 5, other).wait_recv()
@@ -374,14 +381,10 @@
                     make_q(k)
                 debias(k, level, prior_ref, raw_c)
                 send_back(k)
-        for k in mine:
-            if level == 2 or k not in first:
-                extra(k, other).wait_recv()
-            means(k, level)
-            if k // SPLIT == level:
-                own_mean(k).start()
-            else:
-                outward_mean(k, level).start()
+                if k in mine and k not in late_mine:
+                    make_mean(k)
+        for k in late_mine:
+            make_mean(k)
         for y in range(LEVELS):
             for i in range(GROUP):
                 part[y, i] = jnp.sum(acc[y, i], axis=0, keepdims=True)
@@ -389,40 +392,35 @@
             share(level, y, o, flip).start()
         spread_in[spread_slot(level, side, r)] = part[level, r]
 
-        for k in order:
-            across_wait(k, level, True)
-            across_relay(k, level).wait_send()
-            outward_relay(k, level).wait_send()
-            outward_q(k, level).wait_send()
-        for k in sent_extras:
-            extra(k, level).wait_send()
+        across_sent(level)
+        drain(raw_a.at[:, nodes(level == 2)], far_send.at[2])
+        drain(raw_a.at[pl.ds(0, len(sent_extras)), 0], far_send.at[3])
+        drain(raw_b.at[:, nodes(False)], far_send.at[4])
+        drain(q_out, far_send.at[5])
         w_copy(level, 3, beside).wait_send()
         w_copy(level, 4, other).wait_send()
         w_copy(beside, 5, other).wait_send()
         w_copy(other, 6, beside).wait_send()
         w_copy(opp, 7, beside).wait_send()
-        for k in mine:
-            if k // SPLIT == level:
-                own_mean(k).wait()
-            else:
-                outward_mean(k, level).wait_send()
+        drain(avgbuf.at[0], avg_send)
+        drain(avgbuf.at[1], avg_recv)
         gather_spread(level)
-        for y, o, flip in shares(level):
-            share(level, y, o, flip).wait_send()
+        drain(part, s_send.at[1])
+        drain(spread_in.at[pl.ds(0, spread_in.shape[0] - 1)], s_send.at[0])
 
     def outer_role(level):
         beside, other, opp = NEIGHBOUR[level], 3 - level, (level + 2) % LEVELS
-        arrived.clear()
         send_near(first)
         for o in (1, 2, 3):
             w_near(o).start()
         send_near(order[AHEAD:])
         for n, k in enumerate(order):
-            wait_own(k)
+            if k in first:
+                wait_beside(k)
+            wait_near(k)
             to_inner(k, beside).start()
             if n == 0:
-                for o in (1, 2, 3):
-                    w_near(o).wait_recv()
+                near_weights()
                 w_copy(level, 3, beside).start()
         w_copy(beside, 3, beside).wait_recv()
         w_copy(opp, 6, beside).wait_recv()
@@ -432,24 +430,21 @@
             outward_q(k, beside).wait_recv()
             debias(k, level, None, raw_a)
             send_back(k)
-        for k in order:
-            to_inner(k, beside).wait_send()
+        drain(raw_own, far_send.at[0])
         w_copy(level, 3, beside).wait_send()
-        for k in range(SPLIT):
-            outward_mean(k + level * SPLIT, beside).wait_recv()
+        drain(avgbuf.at[0], avg_recv)
         gather_spread(level)
 
     for level in range(LEVELS):
         role = inner_role if level in (1, 2) else outer_role
         pl.when(z == level)(functools.partial(role, level))
 
-    for k in order:
-        for o in (1, 2, 3):
-            near(k, o).wait_send()
-            back(k, o).wait()
-        back_local(k).wait()
-    for o in (1, 2, 3):
-        w_near(o).wait_send()
+    others = pl.ds(0, GROUP - 1)
+    drain(raw_own.at[:, others], near_send)
+    drain(dbuf.at[:, others], back_send)
+    drain(dbuf.at[:, others], back_recv)
+    drain(dbuf.at[:, 0], back_own)
+    drain(wts.at[0, others], w_send.at[0])
     total = spread_in[0]
     for slot in range(1, spread_in.shape[0]):
         total = total + spread_in[slot]
@@ -483,12 +478,10 @@
             pltpu.VMEM((LEVELS, GROUP, 8, LANES), jnp.float32),
             pltpu.VMEM((LEVELS, GROUP, 1, LANES), jnp.float32),
             pltpu.VMEM((4 * GROUP, 1, LANES), jnp.float32),
-            dma((chunks, 3)), dma((chunks, 3)), dma((chunks,)),
-            dma((chunks, 3)), dma((chunks, 3)), dma((chunks,)),
-            dma((AHEAD, GROUP)), dma((AHEAD, GROUP)),
-            dma((chunks, 5)), dma((chunks, 5)),
-            dma((8,)), dma((8,)), dma((LEVELS, GROUP, 2)), dma((4 * GROUP,)),
-            dma((SPLIT,)), dma((SPLIT,)),
+            dma, dma((chunks,)), dma((AHEAD,)), dma, dma, dma, dma,
+            dma((8,)), dma((chunks,)), dma((chunks,)), dma((chunks,)), dma((chunks,)),
+            dma((chunks // 2,)),
+            dma((8,)), dma((8,)), dma((2,)), dma, dma, dma,
         ],
         compiler_params=pltpu.CompilerParams(
             collective_id=0, has_side_effects=True, vmem_limit_bytes=20 << 20),

time: 101 us -> 96.5 us (0.955)
  Pallas kernels: 94.2 us -> 89.3 us
    pallas_call x1, Pallas kernels: 94.2 us -> 89.3 us  [fused(): pl.pallas_call(kernel, out_shape=(jax.ShapeDtypeStruct((1, rows, hidden),...]
where the time goes in v2:
time: 96.5 us; the launch traced here: 96.4 us
  Pallas kernels  89.3 us (93%)
  local copies, waits for them, and re-layouts  4.02 us (4%)
  between operations  3.06 us (3%)
    pallas_call x1, Pallas kernels, fused(): pl.pallas_call(kernel, out_shape=(jax.ShapeDtypeStruct((1, rows, hidden),...  89.3 us
    unnamed x4, local copies, waits for them, and re-layouts  4.02 us

profile of v2, /device:TPU:0, one launch (start us, length us, event | category | flops | bytes accessed | tf_op | source)
XLA Modules:
  0.0 96.4 jit_solution(8778462081680280475)
XLA Ops:
  1.3 0.0 copy-start
  1.3 1.5 %copy-done = bf16[1,64,14336]{2,1,0:T(8,128)(2,1)S(1)} copy-done((bf16[1,64,14336]{2,1,0:T(8,128)(2,1)S(1)}, bf16[1,64,14336]{2,1,0:T(8,128)(2,1)}, u32[]{:S(2)}) %copy-start) | copy-done | bytes 1835032
  2.8 89.3 %shard_map.49 = (f32[1,64,14336]{2,1,0:T(8,128)S(1)}, f32[64,896]{1,0:T(8,128)S(1)}, f32[1]{0:T(128)}) custom-call(bf16[1,64,14336]{2,1,0:T(8,128)(2,1)S(1)} %copy-done, s32[1]{0:T(128)S(6)} %copy.8.w_ref), custom_call_target="tpu_custom_call" | custom-call | tf_op jit(solution)/shard_map/pallas_call | solution.py:463
  92.1 1.8 %copy.9 = f32[1,64,14336]{2,1,0:T(8,128)} copy(f32[1,64,14336]{2,1,0:T(8,128)S(1)} %get-tuple-element.6) | data formatting | bytes 7340032
  93.9 0.7 copy.10
Async XLA Ops:
  1.3 1.5 %copy-start = (bf16[1,64,14336]{2,1,0:T(8,128)(2,1)S(1)}, bf16[1,64,14336]{2,1,0:T(8,128)(2,1)}, u32[]{:S(2)}) copy-start(bf16[1,64,14336]{2,1,0:T(8,128)(2,1)} %p_ref.1) | copy-start | bytes 5505028

commit v3 on v2

--- a/solution.py
+++ b/solution.py
@@ -12,8 +12,9 @@
 LEVELS = 4
 SPLIT = 4
 LANES = 128
+FIRST = 2
 AHEAD = 2
-LATE = 4
+LATE = 6
 NEIGHBOUR = (1, 0, 3, 2)
 
 
@@ -36,7 +37,7 @@
     lows = list(range(middle))
     highs = list(range(middle + SPLIT, chunks)) + list(range(middle, middle + SPLIT))
     order = [k for pair in zip(lows, highs) for k in pair]
-    first = order[:AHEAD]
+    first = order[:FIRST]
 
     def peer(o):
         y = 1 - half if o & 2 else half
@@ -228,12 +229,17 @@
     def all_own(k, source):
         return source == 1 or (k in first and k < middle)
 
-    def send_piece(k, o, source):
-        start = piece(k, o, source).start
+    def pair(k, part_of, source):
+        return remote(raw_own.at[k, part_of], raw_b.at[k, part_of],
+                      far_send.at[6 if all_own(k, source) else 7], own_recv.at[k],
+                      dev(3 - source, r))
+
+    def send_pair(k, chip, source):
         if all_own(k, source):
-            start()
+            pair(k, pl.ds(2 * chip, 2), source).start()
         else:
-            pl.when(peer(o) != 0)(start)
+            pl.when(chip == 0)(pair(k, pl.ds(1, 1), source).start)
+            pl.when(chip == 1)(pair(k, pl.ds(2, 2), source).start)
 
     def across(k, source):
         part_of = nodes(source == 1)
@@ -244,12 +250,12 @@
         drain(raw_b.at[k, nodes(all_own(k, source))], own_recv.at[k])
 
     def across_sent(source):
-        drain(raw_own.at[pl.ds(0, chunks - AHEAD), nodes(source == 1)], far_send.at[1])
+        drain(raw_own.at[pl.ds(0, chunks - FIRST), nodes(source == 1)], far_send.at[1])
         if source == 1:
-            drain(raw_own.at[pl.ds(0, AHEAD)], far_send.at[6])
+            drain(raw_own.at[pl.ds(0, FIRST)], far_send.at[6])
         else:
-            drain(raw_own.at[pl.ds(0, AHEAD // 2)], far_send.at[6])
-            drain(raw_own.at[pl.ds(0, AHEAD // 2), nodes(False)], far_send.at[7])
+            drain(raw_own.at[pl.ds(0, FIRST // 2)], far_send.at[6])
+            drain(raw_own.at[pl.ds(0, FIRST // 2), nodes(False)], far_send.at[7])
 
     def across_relay(k, source):
         part_of = nodes(source == 2)
@@ -331,24 +337,30 @@
             else:
                 outward_mean(k, level).start()
 
-        for k in first:
-            send_piece(k, 0, level)
+        lone = [k for k in first if all_own(k, level)][:FIRST // 2]
+        for k in lone:
+            piece(k, 0, level).start()
         send_near(first)
         for o in (1, 2, 3):
             w_near(o).start()
-        send_near(order[AHEAD:])
+        send_near(order[FIRST:])
         for k in first:
             wait_beside(k)
-            send_piece(k, 1, level)
+            if k in lone:
+                piece(k, 1, level).start()
+            else:
+                send_pair(k, half, level)
         for n, k in enumerate(first):
             wait_near(k)
-            for o in (2, 3):
-                send_piece(k, o, level)
+            send_pair(k, 1 - half, level)
             if n == 0:
                 near_weights()
                 w_copy(level, 3, beside).start()
                 w_copy(level, 4, other).start()
 
+        for k in order[FIRST:AHEAD]:
+            wait_near(k)
+            across(k, level).start()
         for t in range(chunks + 2):
             if t + AHEAD < chunks:
                 wait_near(order[t + AHEAD])
@@ -413,7 +425,7 @@
         send_near(first)
         for o in (1, 2, 3):
             w_near(o).start()
-        send_near(order[AHEAD:])
+        send_near(order[FIRST:])
         for n, k in enumerate(order):
             if k in first:
                 wait_beside(k)
@@ -478,14 +490,37 @@
             pltpu.VMEM((LEVELS, GROUP, 8, LANES), jnp.float32),
             pltpu.VMEM((LEVELS, GROUP, 1, LANES), jnp.float32),
             pltpu.VMEM((4 * GROUP, 1, LANES), jnp.float32),
-            dma, dma((chunks,)), dma((AHEAD,)), dma, dma, dma, dma,
+            dma, dma((chunks,)), dma((FIRST,)), dma, dma, dma, dma,
             dma((8,)), dma((chunks,)), dma((chunks,)), dma((chunks,)), dma((chunks,)),
             dma((chunks // 2,)),
             dma((8,)), dma((8,)), dma((2,)), dma, dma, dma,
         ],
         compiler_params=pltpu.CompilerParams(
             collective_id=0, has_side_effects=True, vmem_limit_bytes=20 << 20),
-    )(params, weights)
+    )(pltpu.with_memory_space_constraint(params, pltpu.HBM), weights)
+    def place(d_in, a_in, d_out, a_out, sems):
+        copies = []
+        parts = 8
+        step = rows // parts
+        for n in range(parts):
+            part_of = pl.ds(n * step, step)
+            copies.append(pltpu.make_async_copy(
+                d_in.at[0, part_of], d_out.at[0, part_of], sems.at[n]))
+        copies.append(pltpu.make_async_copy(a_in, a_out, sems.at[parts]))
+        for copy in copies:
+            copy.start()
+        for copy in copies:
+            copy.wait()
+
+    debiased, average = pl.pallas_call(
+        place,
+        out_shape=(jax.ShapeDtypeStruct(debiased.shape, debiased.dtype),
+                   jax.ShapeDtypeStruct(average.shape, average.dtype)),
+        in_specs=[pl.BlockSpec(memory_space=pl.ANY)] * 2,
+        out_specs=(pl.BlockSpec(memory_space=pl.ANY),) * 2,
+        scratch_shapes=[dma((9,))],
+        compiler_params=pltpu.CompilerParams(vmem_limit_bytes=1 << 20),
+    )(debiased, average)
     return debiased, average, spread
 
 

time: 96.5 us -> 94.8 us (0.982)
  local copies, waits for them, and re-layouts: 4.02 us -> 0 us
  Pallas kernels: 89.3 us -> 91.6 us
    unnamed x4 -> x0, local copies, waits for them, and re-layouts: 4.02 us -> none
    pallas_call x0 -> x1, Pallas kernels: none -> 1.98 us  [fused(): pl.pallas_call(place, out_shape=(jax.ShapeDtypeStruct(debiased.shape, deb...]
where the time goes in v3:
time: 94.8 us; the launch traced here: 94.6 us
  Pallas kernels  91.6 us (97%)
  between operations  3.05 us (3%)
    pallas_call x1, Pallas kernels, fused(): pl.pallas_call(kernel, out_shape=(jax.ShapeDtypeStruct((1, rows, hidden),...  89.6 us
    pallas_call x1, Pallas kernels, fused(): pl.pallas_call(place, out_shape=(jax.ShapeDtypeStruct(debiased.shape, deb...  1.98 us

profile of v3, /device:TPU:0, one launch (start us, length us, event | category | flops | bytes accessed | tf_op | source)
XLA Modules:
  0.0 94.6 jit_solution(10723182121660242604)
XLA Ops:
  1.3 89.6 %shard_map.49 = (f32[1,64,14336]{2,1,0:T(8,128)S(1)}, f32[64,896]{1,0:T(8,128)S(1)}, f32[1]{0:T(128)}) custom-call(bf16[1,64,14336]{2,1,0:T(8,128)(2,1)} %p_ref.1, s32[1]{0:T(128)S(6)} %copy.6.w_ref), custom_call_target="tpu_custom_call" | custom-call | tf_op jit(solution)/shard_map/pallas_call | solution.py:475
  90.9 2.0 %shard_map.50 = (f32[1,64,14336]{2,1,0:T(8,128)}, f32[64,896]{1,0:T(8,128)}) custom-call(f32[1,64,14336]{2,1,0:T(8,128)S(1)} %get-tuple-element.8.d_in, f32[64,896]{1,0:T(8,128)S(1)} %get-tuple-element.9.a_in), custom_call_target="tpu_custom_call" | custom-call | tf_op jit(solution)/shard_map/pallas_call | solution.py:515

commit v4 on v3

--- a/solution.py
+++ b/solution.py
@@ -14,16 +14,17 @@
 LANES = 128
 FIRST = 2
 AHEAD = 2
-LATE = 6
+LATE = (0, 1, 6)
+TAPER = 2
 NEIGHBOUR = (1, 0, 3, 2)
 
 
 def kernel(p_ref, w_ref, out_ref, avg_ref, spread_ref,
            raw_own, raw_a, raw_b, raw_c, q_in, q_out, dbuf, avgbuf,
            wts, acc, part, spread_in,
-           near_send, near_recv, beside_recv, own_sem, back_send, back_recv, back_own,
+           near_send, near_recv, beside_recv, own_sem, back_send, back_recv,
            far_send, own_recv, relay_recv, beside_in, q_recv, extra_recv,
-           w_send, w_recv, s_send, s_recv, avg_send, avg_recv):
+           w_send, w_recv, s_send, s_recv, avg_send, avg_recv, ready):
     node = lax.axis_index("node")
     side = lax.axis_index("blk")
     z = node // GROUP
@@ -38,6 +39,17 @@
     highs = list(range(middle + SPLIT, chunks)) + list(range(middle, middle + SPLIT))
     order = [k for pair in zip(lows, highs) for k in pair]
     first = order[:FIRST]
+    tiles = width // LANES
+    cuts = sorted({0, tiles - TAPER * 2, tiles - TAPER, tiles} & set(range(tiles + 1)))
+
+    def units(k):
+        if k != order[-1]:
+            return [(k, 0, tiles, k)]
+        spare = [k] + list(range(chunks, chunks + 2))
+        return [(k, lo, hi - lo, sem) for lo, hi, sem in zip(cuts, cuts[1:], spare)]
+
+    def lanes(unit):
+        return pl.ds(unit[1] * LANES, unit[2] * LANES)
 
     def peer(o):
         y = 1 - half if o & 2 else half
@@ -50,7 +62,6 @@
     inner = jnp.logical_and(z >= 1, z <= 2)
     mate = 3 - z
     nb = (z // 2) * 2 + 1 - z % 2
-    inner_count = (1 - z // 3) * ((z + 2) // 3)
 
     def remote(src, dst, ssem, rsem, device):
         return pltpu.make_async_remote_copy(
@@ -75,11 +86,11 @@
     for o in (1, 2, 3):
         greet(dev(z, peer(o)))
     greet({"blk": 1 - side})
-    greet(dev(nb, r))
 
     @pl.when(inner)
     def _():
         greet(dev(mate, r))
+        greet(dev(nb, r))
 
     def local_in(k):
         return pltpu.make_async_copy(
@@ -90,7 +101,7 @@
     wts[z, r] = jnp.full((8, LANES), w_ref[0].astype(jnp.float32))
     acc[...] = jnp.zeros_like(acc)
 
-    pl.semaphore_wait(barrier, 5 + inner_count)
+    pl.semaphore_wait(barrier, 5)
     drain(raw_own.at[:, 0], own_sem)
 
     def w_near(o):
@@ -130,18 +141,18 @@
     def columns(j):
         return pl.ds(pl.multiple_of(j * LANES, LANES), LANES)
 
-    def back(k, o):
-        return remote(dbuf.at[k, peer(o)], out_ref.at[0, own_slice(k), block(k, r)],
+    def out_block(unit):
+        k, lo, count, _ = unit
+        start = ((k // SPLIT) * GROUP + r) * width + lo * LANES
+        return out_ref.at[0, own_slice(k), pl.ds(pl.multiple_of(start, LANES), count * LANES)]
+
+    def back(unit, o):
+        return remote(dbuf.at[unit[0], peer(o), :, lanes(unit)], out_block(unit),
                       back_send, back_recv, dev(z, peer(o)))
 
-    def back_local(k):
-        return pltpu.make_async_copy(
-            dbuf.at[k, r], out_ref.at[0, own_slice(k), block(k, r)], back_own)
-
-    def send_back(k):
+    def send_back(unit):
         for o in (2, 3, 1):
-            back(k, o).start()
-        back_local(k).start()
+            back(unit, o).start()
 
     def group_weight(zz):
         return row(zz, 0) + row(zz, 1) + row(zz, 2) + row(zz, 3)
@@ -164,7 +175,8 @@
         sums = [head + prior for head in heads]
         return [sums[i] + tails[i + 1] for i in range(GROUP - 1)] + [sums[-1]]
 
-    def debias(k, level, prior_ref, tail_ref):
+    def debias(unit, level, prior_ref, tail_ref):
+        k, lo, count, _ = unit
         opp, prior_level = (level + 2) % LEVELS, (level + 3) % LEVELS
         scales = scales_of(level)
 
@@ -178,14 +190,17 @@
             tail = [None] + [value(tail_ref, k, opp, i, cols) for i in range(1, GROUP)]
             for i, total in enumerate(window(own, tail, prior)):
                 dbuf[k, i, :, cols] = total * scales[i]
+            start = ((k // SPLIT) * GROUP + r) * width + j * LANES
+            place = pl.ds(pl.multiple_of(start, LANES), LANES)
+            out_ref[0, own_slice(k), place] = dbuf[k, r, :, cols]
             return carry
 
-        lax.fori_loop(0, width // LANES, step, 0)
+        lax.fori_loop(lo, lo + count, step, 0)
 
     def means(k, level):
         refs = {level: raw_own, NEIGHBOUR[level]: raw_a, 3 - level: raw_b,
                 (level + 2) % LEVELS: raw_c}
-        slot = 1 if k // SPLIT == level else 0
+        own_average = k // SPLIT == level
         whole = 1.0 / (group_weight(0) + group_weight(1) + group_weight(2) + group_weight(3))
         scales = [scales_of(y) for y in range(LEVELS)]
 
@@ -193,14 +208,19 @@
             cols = columns(j)
             groups = [group_sum(refs[y], k, y, cols) for y in range(LEVELS)]
             mean = ((groups[0] + groups[1]) + (groups[2] + groups[3])) * whole
-            avgbuf[slot, own_slice(k), cols] = mean
+            (avg_ref if own_average else avgbuf)[own_slice(k), cols] = mean
             fresh = []
             for y in range(LEVELS):
                 far = (y + 2) % LEVELS
-                own = [value(refs[y], k, y, i, cols) for i in range(GROUP)]
-                tail = [None] + [value(refs[far], k, far, i, cols) for i in range(1, GROUP)]
-                for i, total in enumerate(window(own, tail, groups[(y + 3) % LEVELS])):
-                    gap = total * scales[y][i] - mean
+                if y == level:
+                    results = [dbuf[k, i, :, cols] for i in range(GROUP)]
+                else:
+                    own = [value(refs[y], k, y, i, cols) for i in range(GROUP)]
+                    tail = [None] + [value(refs[far], k, far, i, cols) for i in range(1, GROUP)]
+                    totals = window(own, tail, groups[(y + 3) % LEVELS])
+                    results = [total * scale for total, scale in zip(totals, scales[y])]
+                for i in range(GROUP):
+                    gap = results[i] - mean
                     gap = gap * gap
                     fold = gap[0:8]
                     for e in range(8, rows, 8):
@@ -257,10 +277,10 @@
             drain(raw_own.at[pl.ds(0, FIRST // 2)], far_send.at[6])
             drain(raw_own.at[pl.ds(0, FIRST // 2), nodes(False)], far_send.at[7])
 
-    def across_relay(k, source):
-        part_of = nodes(source == 2)
-        return remote(raw_a.at[k, part_of], raw_c.at[k, part_of], far_send.at[2],
-                      relay_recv.at[k], dev(3 - source, r))
+    def across_relay(unit, source):
+        place = (unit[0], nodes(source == 2), slice(None), lanes(unit))
+        return remote(raw_a.at[place], raw_c.at[place], far_send.at[2],
+                      relay_recv.at[unit[3]], dev(3 - source, r))
 
     def extra(k, source):
         if source == 1:
@@ -275,17 +295,14 @@
         return remote(raw_b.at[k, part_of], raw_a.at[k, part_of], far_send.at[4],
                       beside_in.at[k], dev(NEIGHBOUR[source], r))
 
-    def outward_q(k, source):
-        return remote(q_out.at[k], q_in.at[k], far_send.at[5], q_recv.at[k],
-                      dev(NEIGHBOUR[source], r))
+    def outward_q(unit, source):
+        place = (unit[0], slice(None), lanes(unit))
+        return remote(q_out.at[place], q_in.at[place], far_send.at[5],
+                      q_recv.at[unit[3]], dev(NEIGHBOUR[source], r))
 
     def outward_mean(k, source):
-        return remote(avgbuf.at[0, own_slice(k)], avg_ref.at[own_slice(k)],
+        return remote(avgbuf.at[own_slice(k)], avg_ref.at[own_slice(k)],
                       avg_send, avg_recv, dev(NEIGHBOUR[source], r))
-
-    def own_mean(k):
-        return pltpu.make_async_copy(
-            avgbuf.at[1, own_slice(k)], avg_ref.at[own_slice(k)], avg_recv)
 
     def w_copy(level, slot, target):
         return remote(wts.at[level], wts.at[level], w_send.at[slot], w_recv.at[slot],
@@ -312,12 +329,13 @@
         beside, other, opp = NEIGHBOUR[level], 3 - level, (level + 2) % LEVELS
         sent_extras = [k for k in (highs if level == 1 else lows)
                        if level == 1 or k not in first]
-        late_sent = sent_extras[-LATE:]
+        late_sent = sent_extras[len(sent_extras) - LATE[level]:]
         mine = lows if level == 1 else highs
-        late_mine = mine[-LATE:]
+        late_mine = mine[len(mine) - LATE[other]:]
         prior_ref = raw_a if level == 1 else raw_b
 
-        def make_q(k):
+        def make_q(unit):
+            k, lo, count, _ = unit
             src, zz = (raw_c, opp) if level == 1 else (raw_own, level)
 
             def step(j, carry):
@@ -325,16 +343,14 @@
                 q_out[k, :, cols] = group_sum(src, k, zz, cols)
                 return carry
 
-            lax.fori_loop(0, width // LANES, step, 0)
-            outward_q(k, level).start()
+            lax.fori_loop(lo, lo + count, step, 0)
+            outward_q(unit, level).start()
 
         def make_mean(k):
             if level == 2 or k not in first:
                 extra(k, other).wait_recv()
             means(k, level)
-            if k // SPLIT == level:
-                own_mean(k).start()
-            else:
+            if k // SPLIT != level:
                 outward_mean(k, level).start()
 
         lone = [k for k in first if all_own(k, level)][:FIRST // 2]
@@ -355,7 +371,6 @@
             send_pair(k, 1 - half, level)
             if n == 0:
                 near_weights()
-                w_copy(level, 3, beside).start()
                 w_copy(level, 4, other).start()
 
         for k in order[FIRST:AHEAD]:
@@ -368,10 +383,13 @@
             if t < chunks:
                 k = order[t]
                 to_inner(k, beside).wait_recv()
-                across_relay(k, level).start()
+                for unit in units(k):
+                    across_relay(unit, level).start()
                 if k in sent_extras and k not in late_sent:
                     extra(k, level).start()
                 if t == 0:
+                    pl.semaphore_wait(ready, 1)
+                    w_copy(level, 3, beside).start()
                     w_copy(beside, 3, beside).wait_recv()
                     w_copy(beside, 5, other).start()
                     w_copy(level, 4, other).wait_recv()
@@ -380,7 +398,8 @@
                     for e in late_sent:
                         extra(e, level).start()
                 if level == 2:
-                    make_q(k)
+                    for unit in units(k):
+                        make_q(unit)
                 across_wait(k, other)
                 outward_relay(k, level).start()
             if t == 2:
@@ -388,11 +407,12 @@
                 w_copy(opp, 7, beside).start()
             if t >= 2:
                 k = order[t - 2]
-                across_relay(k, other).wait_recv()
-                if level == 1:
-                    make_q(k)
-                debias(k, level, prior_ref, raw_c)
-                send_back(k)
+                for unit in units(k):
+                    across_relay(unit, other).wait_recv()
+                    if level == 1:
+                        make_q(unit)
+                    debias(unit, level, prior_ref, raw_c)
+                    send_back(unit)
                 if k in mine and k not in late_mine:
                     make_mean(k)
         for k in late_mine:
@@ -414,14 +434,15 @@
         w_copy(beside, 5, other).wait_send()
         w_copy(other, 6, beside).wait_send()
         w_copy(opp, 7, beside).wait_send()
-        drain(avgbuf.at[0], avg_send)
-        drain(avgbuf.at[1], avg_recv)
+        drain(avgbuf, avg_send)
         gather_spread(level)
         drain(part, s_send.at[1])
         drain(spread_in.at[pl.ds(0, spread_in.shape[0] - 1)], s_send.at[0])
 
     def outer_role(level):
         beside, other, opp = NEIGHBOUR[level], 3 - level, (level + 2) % LEVELS
+        pl.semaphore_signal(ready, inc=1, device_id=dev(beside, r),
+                            device_id_type=pl.DeviceIdType.MESH)
         send_near(first)
         for o in (1, 2, 3):
             w_near(o).start()
@@ -439,12 +460,13 @@
         w_copy(other, 7, beside).wait_recv()
         for k in order:
             outward_relay(k, beside).wait_recv()
-            outward_q(k, beside).wait_recv()
-            debias(k, level, None, raw_a)
-            send_back(k)
+            for unit in units(k):
+                outward_q(unit, beside).wait_recv()
+                debias(unit, level, None, raw_a)
+                send_back(unit)
         drain(raw_own, far_send.at[0])
         w_copy(level, 3, beside).wait_send()
-        drain(avgbuf.at[0], avg_recv)
+        drain(avgbuf, avg_recv)
         gather_spread(level)
 
     for level in range(LEVELS):
@@ -455,7 +477,6 @@
     drain(raw_own.at[:, others], near_send)
     drain(dbuf.at[:, others], back_send)
     drain(dbuf.at[:, others], back_recv)
-    drain(dbuf.at[:, 0], back_own)
     drain(wts.at[0, others], w_send.at[0])
     total = spread_in[0]
     for slot in range(1, spread_in.shape[0]):
@@ -480,20 +501,21 @@
             jax.ShapeDtypeStruct((1,), jnp.float32),
         ),
         in_specs=[pl.BlockSpec(memory_space=pltpu.HBM), pl.BlockSpec(memory_space=pltpu.SMEM)],
-        out_specs=(pl.BlockSpec(memory_space=pl.ANY), pl.BlockSpec(memory_space=pl.ANY),
+        out_specs=(pl.BlockSpec(memory_space=pltpu.VMEM), pl.BlockSpec(memory_space=pltpu.VMEM),
                    pl.BlockSpec(memory_space=pltpu.SMEM)),
         scratch_shapes=[
             raw, raw, raw, raw, q, q,
             pltpu.VMEM((chunks, GROUP, piece_rows, width), jnp.float32),
-            pltpu.VMEM((2, rows, width), jnp.float32),
+            pltpu.VMEM((rows, width), jnp.float32),
             pltpu.VMEM((LEVELS, GROUP, 8, LANES), jnp.float32),
             pltpu.VMEM((LEVELS, GROUP, 8, LANES), jnp.float32),
             pltpu.VMEM((LEVELS, GROUP, 1, LANES), jnp.float32),
             pltpu.VMEM((4 * GROUP, 1, LANES), jnp.float32),
-            dma, dma((chunks,)), dma((FIRST,)), dma, dma, dma, dma,
-            dma((8,)), dma((chunks,)), dma((chunks,)), dma((chunks,)), dma((chunks,)),
+            dma, dma((chunks,)), dma((FIRST,)), dma, dma, dma,
+            dma((8,)), dma((chunks,)), dma((chunks + 2,)), dma((chunks,)), dma((chunks + 2,)),
             dma((chunks // 2,)),
             dma((8,)), dma((8,)), dma((2,)), dma, dma, dma,
+            pltpu.SemaphoreType.REGULAR,
         ],
         compiler_params=pltpu.CompilerParams(
             collective_id=0, has_side_effects=True, vmem_limit_bytes=20 << 20),

time: 94.8 us -> 94.6 us (level)
  no operation moved by 1% of the time
where the time goes in v4:
time: 94.6 us; the launch traced here: 94.4 us
  Pallas kernels  91.3 us (97%)
  between operations  3.05 us (3%)
    pallas_call x1, Pallas kernels, fused(): pl.pallas_call(kernel, out_shape=(jax.ShapeDtypeStruct((1, rows, hidden),...  89.3 us
    pallas_call x1, Pallas kernels, fused(): pl.pallas_call(place, out_shape=(jax.ShapeDtypeStruct(debiased.shape, deb...  1.98 us

profile of v4, /device:TPU:0, one launch (start us, length us, event | category | flops | bytes accessed | tf_op | source)
XLA Modules:
  0.0 94.4 jit_solution(8836153453564613621)
XLA Ops:
  1.3 89.3 %shard_map.49 = (f32[1,64,14336]{2,1,0:T(8,128)S(1)}, f32[64,896]{1,0:T(8,128)S(1)}, f32[1]{0:T(128)}) custom-call(bf16[1,64,14336]{2,1,0:T(8,128)(2,1)} %p_ref.1, s32[1]{0:T(128)S(6)} %copy.6.w_ref), custom_call_target="tpu_custom_call" | custom-call | tf_op jit(solution)/shard_map/pallas_call | solution.py:496
  90.6 2.0 %shard_map.50 = (f32[1,64,14336]{2,1,0:T(8,128)}, f32[64,896]{1,0:T(8,128)}) custom-call(f32[1,64,14336]{2,1,0:T(8,128)S(1)} %get-tuple-element.8.d_in, f32[64,896]{1,0:T(8,128)S(1)} %get-tuple-element.9.a_in), custom_call_target="tpu_custom_call" | custom-call | tf_op jit(solution)/shard_map/pallas_call | solution.py:537
